TPU v7x, 256 devices: a whole 4x4x8 slice. The times are simulated.
256 devices in a mesh: dom: 32 (over y, x, z_hi), orb: 8 (over z_lo, core).
Axes of the slice: x: 4, y: 4, z: 8 (z_hi: 2, z_lo: 4; z = z_hi * 4 + z_lo), core: 2. Of those that a mesh axis runs over, the one named last changes fastest.
Arguments:
- orbitals: float32 [16, 256, 64, 128], P('orb', 'dom'), may hold values from -10.8 to 10.8
- initial_guess: float32 [16, 256, 64, 128], P('orb', 'dom'), may hold values from -350 to 350
- potential: float32 [256, 64, 128], P('dom'), may hold values from 0.1 to 2
- perturbation: float32 [256, 64, 128], P('dom'), may hold values from -6 to 6
- level_shifts: float32 [16], replicated, may hold values from 0.05 to 2
- assignment: int32 [16], P('orb'), may hold values from 0 to 15, each once
Outputs:
- updated_response: float32 [16, 256, 64, 128], P('orb', 'dom')
Inputs may be any that keep to these rules, and one draw needn't show every extreme that they name: `assignment`: every energy index appears in exactly one slot.
All inputs are finite; a program needn't handle non-finite values.
Results may differ from a plain program's by a relative error of at most 0.0003.
Values sent between devices are 32-bit elements; how exact they have to be, the bound alone decides.
A program may use at most 128 MiB of HBM per device.

v0:
```python
import functools

import jax
import jax.numpy as jnp
from jax import lax
from jax.experimental import pallas as pl
from jax.experimental.pallas import tpu as pltpu
from jax.sharding import PartitionSpec as P

OMEGA = 0.8
KINETIC = 8.0
MESH = pl.DeviceIdType.MESH
F32 = jnp.float32


def turn(x, shift, axis):
    return pltpu.roll(x, shift % x.shape[axis], axis)


def ring(x, step):
    ya, za = x.ndim - 2, x.ndim - 1
    return (turn(x, 1, ya) + turn(x, -1, ya)) + (turn(x, step, za) + turn(x, -step, za))


def lane_bit(shape, bit):
    return (lax.broadcasted_iota(jnp.int32, shape, len(shape) - 1) & bit) == 0


def pair(first, second, bit):
    za = first.ndim - 1
    return jnp.where(
        lane_bit(first.shape, bit), first + turn(first, -bit, za), second + turn(second, bit, za)
    )


def split(packed, bit):
    za = packed.ndim - 1
    clear = lane_bit(packed.shape, bit)
    return (
        jnp.where(clear, packed, turn(packed, bit, za)),
        jnp.where(clear, turn(packed, -bit, za), packed),
    )


def kernel(
    cells, orb_in, guess_in, pot_in, pert_in, table, slot, out,
    orbs, g, pot, pert, gh, st_out, st_in, c2_out, c2_in, fe_out, fe_in,
    f, w, ea, eb, f1, c1, w1, e1, f2_out, f2_in, rows, gram, part1, part2, coef,
    load_sem, halo_send, halo_recv, wide_send, wide_recv, ag_send, ag_recv,
    gram_send, gram_recv, sum_send, sum_recv,
):
    d = lax.axis_index("dom")
    o = lax.axis_index("orb")
    doms = lax.axis_size("dom")
    layers, half, quarter = 8, 4, 2

    loads = [
        pltpu.make_async_copy(guess_in, g.at[:, pl.ds(1, layers)], load_sem.at[0]),
        pltpu.make_async_copy(orb_in, orbs.at[o], load_sem.at[1]),
        pltpu.make_async_copy(pot_in, pot, load_sem.at[2]),
        pltpu.make_async_copy(pert_in, pert, load_sem.at[3]),
    ]
    for copy in loads:
        copy.start()

    barrier = pltpu.get_barrier_semaphore()
    plane = lax.div(d, 8) * 8
    near = [lax.rem(d + doms + k, doms) for k in (-3, -2, -1, 1, 2, 3)]
    line = [plane + lax.rem(d - plane + k, 8) for k in range(1, 8)]
    far = [lax.rem(d + 8 * k, doms) for k in range(1, 4)]
    chip = lax.div(o, 2)
    mate = o + 1 - 2 * lax.rem(o, 2)
    others = [mate] + [lax.rem(o + 2 * k, 8) for k in range(1, 4)]
    for there in near + line + far:
        pl.semaphore_signal(barrier, inc=1, device_id={"dom": there}, device_id_type=MESH)
    for there in others:
        pl.semaphore_signal(barrier, inc=1, device_id={"orb": there}, device_id_type=MESH)

    shift = [table[slot[i]] for i in range(2)]
    base = [6.0 * KINETIC + s for s in shift]
    zero = jnp.zeros((64, 128), F32)
    for i in range(2):
        g[i, 0] = zero
        g[i, layers + 1] = zero
    for copy in loads:
        copy.wait()

    def start_layer(l, carry):
        p, q = pot[l], pert[l]
        for i in range(2):
            x = g[i, l + 1]
            diag = p + base[i]
            around = ring(x, 1) + (g[i, l] + g[i, l + 2])
            f[i, l + 1] = KINETIC * around - diag * x - q * orbs[o, i, l]
            w[i, l + 1] = OMEGA / diag
        return carry

    lax.fori_loop(0, layers, start_layer, 0)
    for side, (edge, inner) in enumerate(((1, 2), (layers, layers - 1))):
        for i in range(2):
            fe_out[side, 0, i] = f[i, edge]
            fe_out[side, 1, i] = w[i, inner] * f[i, inner]

    for q in range(half):
        t = pot[2 * q] + pot[2 * q + 1]
        rows[q] = pair(t, t, 1)
    for q in range(half):
        c1[q + 2] = 0.125 * (rows[q, pl.ds(0, 32, stride=2)] + rows[q, pl.ds(1, 32, stride=2)])
    even = lane_bit((32, 128), 1)
    st_out[0, pl.ds(0, 64)] = pot[0]
    st_out[1, pl.ds(0, 64)] = pot[layers - 1]
    st_out[0, pl.ds(64, 32)] = jnp.where(even, c1[2], c1[3])
    st_out[1, pl.ds(64, 32)] = jnp.where(even, c1[4], c1[5])
    for q in range(quarter):
        t = c1[2 * q + 2] + c1[2 * q + 3]
        rows[q, pl.ds(0, 32)] = pair(t, t, 2)
    c2 = [
        0.125 * (rows[q, pl.ds(0, 16, stride=2)] + rows[q, pl.ds(1, 16, stride=2)])
        for q in range(quarter)
    ]
    low = lane_bit((16, 128), 2)
    c2_out[...] = jnp.where(low, c2[0], c2[1])

    pl.semaphore_wait(barrier, len(near) + len(line) + len(far) + len(others))

    def to_dom(src, dst, sends, recvs, k, there):
        return pltpu.make_async_remote_copy(
            src_ref=src, dst_ref=dst, send_sem=sends.at[k], recv_sem=recvs.at[k],
            device_id={"dom": there}, device_id_type=MESH,
        )

    below, above = near[2], near[3]
    first = []
    for side, there in ((0, below), (1, above)):
        edge = 1 if side == 0 else layers
        first += [
            to_dom(fe_out.at[side], fe_in.at[1 - side], halo_send, halo_recv, side, there),
            to_dom(g.at[:, edge], gh.at[1 - side], halo_send, halo_recv, 2 + side, there),
            to_dom(st_out.at[side], st_in.at[1 - side], halo_send, halo_recv, 4 + side, there),
        ]
    for copy in first:
        copy.start()
    coarse = [to_dom(c2_out, c2_in.at[5 - k], wide_send, wide_recv, k, near[k]) for k in range(6)]
    for copy in coarse:
        copy.start()

    def hand(block, k, there):
        return pltpu.make_async_remote_copy(
            src_ref=orbs.at[block], dst_ref=orbs.at[block],
            send_sem=ag_send.at[k], recv_sem=ag_recv.at[k],
            device_id={"orb": there}, device_id_type=MESH,
        )

    def up(n):
        return hand(o - 2 * n, n, o + 2)

    def down(n):
        return hand(o + 2 * n, 3 + n, o - 2)

    def over_up(n):
        return hand(o - 2 * n, 6 + n, mate)

    def over_down(n):
        return hand(o + 2 * n, 9 + n, mate)

    across = hand(o, 6, mate)

    def open_gather():
        across.start()

        @pl.when(chip < 3)
        def _():
            up(0).start()

        @pl.when(chip > 0)
        def _():
            down(0).start()

    def relay(n):
        @pl.when(chip >= n)
        def _():
            hand(o - 2 * n, n - 1, o + 2).wait_recv()
            over_up(n).start()

        if n < 3:

            @pl.when((chip >= n) & (chip < 3))
            def _():
                up(n).start()

        @pl.when(chip <= 3 - n)
        def _():
            hand(o + 2 * n, 3 + n - 1, o - 2).wait_recv()
            over_down(n).start()

        if n < 3:

            @pl.when((chip <= 3 - n) & (chip > 0))
            def _():
                down(n).start()

    open_gather()

    for copy in first:
        copy.wait_recv()

    for i in range(2):
        f[i, 1] = f[i, 1] + KINETIC * gh[0, i]
        f[i, layers] = f[i, layers] + KINETIC * gh[1, i]
        for side, (beyond, edge, rim) in enumerate(((0, 1, 0), (layers + 1, layers, 11))):
            f[i, beyond] = fe_in[side, 0, i] + KINETIC * g[i, edge]
            w[i, beyond] = OMEGA / (st_in[side, pl.ds(0, 64)] + base[i])
            ea[i, rim] = fe_in[side, 1, i]
    c1[0], c1[1] = split(st_in[0, pl.ds(64, 32)], 1)
    c1[6], c1[7] = split(st_in[1, pl.ds(64, 32)], 1)

    def begin(l, carry):
        for i in range(2):
            ea[i, l + 1] = w[i, l] * f[i, l]
        return carry

    lax.fori_loop(0, layers + 2, begin, 0)

    def sweep_down(l, carry):
        for i in range(2):
            around = ring(ea[i, l + 1], 1) + (ea[i, l] + ea[i, l + 2])
            eb[i, l + 1] = w[i, l] * ((2.0 - OMEGA) * f[i, l] + KINETIC * around)
        return carry

    lax.fori_loop(0, layers + 2, sweep_down, 0)
    second = [
        to_dom(eb.at[:, 3], eb.at[:, 11], halo_send, halo_recv, 6, below),
        to_dom(eb.at[:, 8], eb.at[:, 0], halo_send, halo_recv, 7, above),
    ]

    def remainder(q, carry):
        total = []
        for i in range(2):
            parts = []
            for h in range(2):
                l = 2 * q + h
                x = eb[i, l + 2]
                around = ring(x, 1) + (eb[i, l + 1] + eb[i, l + 3])
                parts.append(f[i, l + 1] + KINETIC * around - (pot[l] + base[i]) * x)
            total.append(parts[0] + parts[1])
        rows[q] = pair(total[0], total[1], 1)
        return carry

    lax.fori_loop(0, half, remainder, 0)
    for q in range(half):
        f1[q + 2] = 0.125 * (rows[q, pl.ds(0, 32, stride=2)] + rows[q, pl.ds(1, 32, stride=2)])
    third = [
        to_dom(f1.at[pl.ds(2, 2)], f1.at[pl.ds(6, 2)], halo_send, halo_recv, 8, below),
        to_dom(f1.at[pl.ds(4, 2)], f1.at[pl.ds(0, 2)], halo_send, halo_recv, 9, above),
    ]
    for copy in third + second:
        copy.start()
    relay(1)

    k1, k2 = KINETIC / 4, KINETIC / 16
    both = jnp.where(even, shift[0], shift[1])
    for q in range(8):
        w1[q] = OMEGA / (c1[q] + (6.0 * k1 + both))
    for copy in coarse:
        copy.wait_recv()
    both2 = jnp.where(lane_bit((16, 128), 1), shift[0], shift[1])
    c2s = []
    for k in range(3):
        c2s += split(c2_in[k], 2)
    c2s += c2
    for k in range(3, 6):
        c2s += split(c2_in[k], 2)
    w2 = jnp.stack([OMEGA / (c + (6.0 * k2 + both2)) for c in c2s[1:13]])

    for copy in third:
        copy.wait_recv()
    fs, ws = f1[...], w1[...]
    e = ws * fs
    e = ws[1:7] * ((2.0 - OMEGA) * fs[1:7] + k1 * (ring(e[1:7], 2) + (e[:6] + e[2:])))
    e1[pl.ds(2, 6)] = e
    x = e[1:5]
    r = fs[2:6] + k1 * (ring(x, 2) + (e[:4] + e[2:])) - (c1[pl.ds(2, 4)] + (6.0 * k1 + both)) * x
    for q in range(quarter):
        t = r[2 * q] + r[2 * q + 1]
        rows[q, pl.ds(0, 32)] = pair(t, t, 2)
    f2 = [
        0.125 * (rows[q, pl.ds(0, 16, stride=2)] + rows[q, pl.ds(1, 16, stride=2)])
        for q in range(quarter)
    ]
    f2_out[...] = jnp.where(low, f2[0], f2[1])
    fourth = [
        to_dom(f2_out, f2_in.at[5 - k], wide_send, wide_recv, 6 + k, near[k]) for k in range(6)
    ]
    fifth = [
        to_dom(e1.at[pl.ds(4, 2)], e1.at[pl.ds(8, 2)], halo_send, halo_recv, 10, below),
        to_dom(e1.at[pl.ds(4, 2)], e1.at[pl.ds(0, 2)], halo_send, halo_recv, 11, above),
    ]
    for copy in fourth + fifth:
        copy.start()
    relay(2)
    for copy in fourth:
        copy.wait_recv()

    f2s = []
    for k in range(3):
        f2s += split(f2_in[k], 2)
    f2s += f2
    for k in range(3, 6):
        f2s += split(f2_in[k], 2)
    f2v = jnp.stack(f2s[1:13])
    e = w2 * f2v
    for n in range(1, 4):
        inner = slice(n, 12 - n)
        x = e[1:-1]
        e = (1.0 - OMEGA) * x + w2[inner] * (f2v[inner] + k2 * (ring(x, 4) + (e[:-2] + e[2:])))

    for q in range(6):
        rows[q, pl.ds(0, 16, stride=2)] = e[q]
        rows[q, pl.ds(1, 16, stride=2)] = e[q]
    for copy in fifth:
        copy.wait_recv()
    e = jnp.stack([e1[l + 3] + rows[l // 2 + 2, pl.ds(0, 32)] for l in range(-3, 7)])
    for n in range(2):
        inner = slice(n, 8 - n)
        x = e[1:-1]
        e = (1.0 - OMEGA) * x + ws[inner] * (fs[inner] + k1 * (ring(x, 2) + (e[:-2] + e[2:])))
    for q in range(6):
        rows[q, pl.ds(0, 32, stride=2)] = e[q]
        rows[q, pl.ds(1, 32, stride=2)] = e[q]

    for copy in second:
        copy.wait_recv()

    def correct(q, carry):
        fields = split(rows[q], 1)
        for i in range(2):
            for h in range(2):
                ea[i, 2 * q + h] = eb[i, 2 * q + h] + fields[i]
        return carry

    lax.fori_loop(0, 6, correct, 0)
    for copy in second:
        copy.wait_send()

    def sweep_up(l, carry):
        for i in range(2):
            x = ea[i, l + 1]
            around = ring(x, 1) + (ea[i, l] + ea[i, l + 2])
            eb[i, l + 1] = (1.0 - OMEGA) * x + w[i, l] * (f[i, l] + KINETIC * around)
        return carry

    lax.fori_loop(0, layers + 2, sweep_up, 0)

    def sweep_last(l, carry):
        for i in range(2):
            x = eb[i, l + 2]
            around = ring(x, 1) + (eb[i, l + 1] + eb[i, l + 3])
            ea[i, l] = g[i, l + 1] + (
                (1.0 - OMEGA) * x + w[i, l + 1] * (f[i, l + 1] + KINETIC * around)
            )
        return carry

    lax.fori_loop(0, layers, sweep_last, 0)

    relay(3)
    across.wait_recv()
    for n in range(1, 4):

        @pl.when(chip >= n)
        def _():
            over_up(n).wait_recv()

        @pl.when(chip <= 3 - n)
        def _():
            over_down(n).wait_recv()

    def products(n, sums):
        l, r = lax.div(n, 8), pl.ds(pl.multiple_of(lax.rem(n, 8) * 8, 8), 8)
        u = [ea[i, l, r, :] for i in range(2)]
        new = []
        for j in range(16):
            x = orbs[j // 2, j % 2, l, r, :]
            new += [sums[2 * j + i] + x * u[i] for i in range(2)]
        return tuple(new)

    sums = lax.fori_loop(0, 64, products, (jnp.zeros((8, 128), F32),) * 32)
    for m in range(32):
        gram[pl.ds(m, 1), :] = jnp.sum(sums[m], axis=0, keepdims=True)
    diagonal = lax.broadcasted_iota(jnp.int32, (32, 128), 0) == lax.broadcasted_iota(
        jnp.int32, (32, 128), 1
    )

    def lay(column):
        return jnp.sum(jnp.where(diagonal, column, 0.0), axis=0, keepdims=True)

    part1[0] = lay(jnp.sum(gram[...], axis=1, keepdims=True))
    sixth = [
        to_dom(part1.at[0], part1.at[k], gram_send, gram_recv, k - 1, line[k - 1])
        for k in range(1, 8)
    ]
    for copy in sixth:
        copy.start()
    for copy in sixth:
        copy.wait_recv()
    part2[0] = jnp.sum(part1[...], axis=0)
    seventh = [
        to_dom(part2.at[0], part2.at[k], sum_send, sum_recv, k - 1, far[k - 1])
        for k in range(1, 4)
    ]
    for copy in seventh:
        copy.start()
    for copy in seventh:
        copy.wait_recv()
    total = jnp.sum(part2[...], axis=0) * (1.0 / cells)
    coef[...] = jnp.broadcast_to(
        jnp.sum(jnp.where(diagonal, total, 0.0), axis=1, keepdims=True), (32, 128)
    )
    factors = [jnp.broadcast_to(coef[pl.ds(m, 1), :], (8, 128)) for m in range(32)]

    def project(n, carry):
        l, r = lax.div(n, 8), pl.ds(pl.multiple_of(lax.rem(n, 8) * 8, 8), 8)
        lost = [None, None]
        for j in range(16):
            x = orbs[j // 2, j % 2, l, r, :]
            for i in range(2):
                term = factors[2 * j + i] * x
                lost[i] = term if lost[i] is None else lost[i] + term
        for i in range(2):
            eb[i, l, r, :] = ea[i, l, r, :] - lost[i]
        return carry

    lax.fori_loop(0, 64, project, 0)
    store = pltpu.make_async_copy(eb.at[:, pl.ds(0, layers)], out, load_sem.at[0])
    store.start()

    for copy in first + coarse + third + fourth + fifth + sixth + seventh:
        copy.wait_send()
    across.wait_send()
    for n in range(3):

        @pl.when((chip >= n) & (chip < 3))
        def _():
            up(n).wait_send()

        @pl.when((chip <= 3 - n) & (chip > 0))
        def _():
            down(n).wait_send()

    for n in range(1, 4):

        @pl.when(chip >= n)
        def _():
            over_up(n).wait_send()

        @pl.when(chip <= 3 - n)
        def _():
            over_down(n).wait_send()

    store.wait()


def on_device(orbitals, initial_guess, potential, perturbation, level_shifts, assignment):
    cells = orbitals.shape[1] * lax.axis_size("dom") * orbitals.shape[2] * orbitals.shape[3]
    dma = pltpu.SemaphoreType.DMA
    vmem = pltpu.VMEM

    def field(*shape):
        return vmem(shape, F32)

    anywhere = pl.BlockSpec(memory_space=pl.ANY)
    scalars = pl.BlockSpec(memory_space=pltpu.SMEM)
    return pl.pallas_call(
        functools.partial(kernel, cells),
        out_shape=jax.ShapeDtypeStruct(orbitals.shape, F32),
        in_specs=[anywhere] * 4 + [scalars] * 2,
        out_specs=anywhere,
        scratch_shapes=[
            field(8, 2, 8, 64, 128),
            field(2, 10, 64, 128),
            field(8, 64, 128),
            field(8, 64, 128),
            field(2, 2, 64, 128),
            field(2, 96, 128),
            field(2, 96, 128),
            field(16, 128),
            field(6, 16, 128),
            field(2, 2, 2, 64, 128),
            field(2, 2, 2, 64, 128),
            field(2, 10, 64, 128),
            field(2, 10, 64, 128),
            field(2, 12, 64, 128),
            field(2, 12, 64, 128),
            field(8, 32, 128),
            field(8, 32, 128),
            field(8, 32, 128),
            field(10, 32, 128),
            field(16, 128),
            field(6, 16, 128),
            field(6, 64, 128),
            field(32, 128),
            field(8, 1, 128),
            field(4, 1, 128),
            field(32, 128),
            dma((4,)),
            dma((12,)),
            dma((12,)),
            dma((12,)),
            dma((12,)),
            dma((13,)),
            dma((13,)),
            dma((7,)),
            dma((7,)),
            dma((3,)),
            dma((3,)),
        ],
        compiler_params=pltpu.CompilerParams(
            collective_id=0, has_side_effects=True, vmem_limit_bytes=32 << 20
        ),
        name="sternheimer",
    )(orbitals, initial_guess, potential, perturbation, level_shifts, assignment)


def solution(mesh):
    in_specs = (
        P("orb", "dom", None, None),
        P("orb", "dom", None, None),
        P("dom", None, None),
        P("dom", None, None),
        P(),
        P("orb"),
    )
    out_specs = P("orb", "dom", None, None)
    return jax.shard_map(
        on_device, mesh=mesh, in_specs=in_specs, out_specs=out_specs, check_vma=False
    )
```

profile of v0, /device:TPU:1, one launch (start us, length us, event | category | flops | bytes accessed | tf_op | source)
XLA Modules:
  0.0 100.6 jit_solution(6820206800970642897)
XLA Ops:
  0.0 0.0 copy-start
  0.0 1.0 %copy-done = f32[2,8,64,128]{3,2,1,0:T(8,128)S(1)} copy-done((f32[2,8,64,128]{3,2,1,0:T(8,128)S(1)}, f32[2,8,64,128]{3,2,1,0:T(8,128)}, u32[]{:S(2)}) %copy-start) | copy-done | bytes 524312
  1.0 0.0 copy-start.1
  1.0 1.0 %copy-done.1 = f32[2,8,64,128]{3,2,1,0:T(8,128)S(1)} copy-done((f32[2,8,64,128]{3,2,1,0:T(8,128)S(1)}, f32[2,8,64,128]{3,2,1,0:T(8,128)}, u32[]{:S(2)}) %copy-start.1) | copy-done | bytes 524312
  2.1 0.0 copy-start.2
  2.1 0.9 copy-done.2
  3.0 0.0 copy-start.3
  3.0 0.9 copy-done.3
  4.0 0.0 copy-start.4
  4.0 0.7 copy-done.4
  4.6 0.0 copy-start.5
  4.6 0.7 copy-done.5
  5.3 94.5 %sternheimer.1 = f32[2,8,64,128]{3,2,1,0:T(8,128)S(1)} custom-call(f32[2,8,64,128]{3,2,1,0:T(8,128)S(1)} %copy-done, f32[2,8,64,128]{3,2,1,0:T(8,128)S(1)} %copy-done.1, f32[8,64,128]{2,1,0:T(8,128)S(1)} %copy-done.2, f32[8,64,128]{2,1,0:T(8,128)S(1)} %copy-done.3, f32[16]{0:T(128)S(1)} %copy-done.4, s32[2]{0:T(128)S(1)} %copy-done.5), custom_call_target="tpu_custom_call" | custom-call | tf_op jit(solution)/shard_map/sternheimer/pallas_call | solution.py:472
  99.8 0.8 copy.8
Async XLA Ops:
  0.0 1.0 %copy-start = (f32[2,8,64,128]{3,2,1,0:T(8,128)S(1)}, f32[2,8,64,128]{3,2,1,0:T(8,128)}, u32[]{:S(2)}) copy-start(f32[2,8,64,128]{3,2,1,0:T(8,128)} %orb_in.1) | copy-start | bytes 1572868
  1.0 1.0 %copy-start.1 = (f32[2,8,64,128]{3,2,1,0:T(8,128)S(1)}, f32[2,8,64,128]{3,2,1,0:T(8,128)}, u32[]{:S(2)}) copy-start(f32[2,8,64,128]{3,2,1,0:T(8,128)} %guess_in.1) | copy-start | bytes 1572868
  2.1 0.9 copy-start.2
  3.0 0.9 copy-start.3
  4.0 0.7 copy-start.4
  4.6 0.7 copy-start.5
where the time goes:
time: 101 us
  Pallas kernels  94.5 us (94%)
  local copies, waits for them, and re-layouts  6.09 us (6%)
    pallas_call x1, Pallas kernels, on_device(): pl.pallas_call(functools.partial(kernel, cells), out_shape=jax.ShapeDtype...  94.5 us
    unnamed x13, local copies, waits for them, and re-layouts  6.09 us

commit v1 on v0

--- a/solution.py
+++ b/solution.py
@@ -45,9 +45,9 @@
 def kernel(
     cells, orb_in, guess_in, pot_in, pert_in, table, slot, out,
     orbs, g, pot, pert, gh, st_out, st_in, c2_out, c2_in, fe_out, fe_in,
-    f, w, ea, eb, f1, c1, w1, e1, f2_out, f2_in, rows, gram, part1, part2, coef,
+    f, w, ea, eb, f1, c1, w1, e1, f2_out, f2_in, rows, gram, part, coef,
     load_sem, halo_send, halo_recv, wide_send, wide_recv, ag_send, ag_recv,
-    gram_send, gram_recv, sum_send, sum_recv,
+    gram_send, gram_recv,
 ):
     d = lax.axis_index("dom")
     o = lax.axis_index("orb")
@@ -64,14 +64,12 @@
         copy.start()
 
     barrier = pltpu.get_barrier_semaphore()
-    plane = lax.div(d, 8) * 8
     near = [lax.rem(d + doms + k, doms) for k in (-3, -2, -1, 1, 2, 3)]
-    line = [plane + lax.rem(d - plane + k, 8) for k in range(1, 8)]
-    far = [lax.rem(d + 8 * k, doms) for k in range(1, 4)]
-    chip = lax.div(o, 2)
-    mate = o + 1 - 2 * lax.rem(o, 2)
+    rest = [lax.rem(d + k, doms) for k in range(1, doms)]
+    chip, core = lax.div(o, 2), lax.rem(o, 2)
+    mate = o + 1 - 2 * core
     others = [mate] + [lax.rem(o + 2 * k, 8) for k in range(1, 4)]
-    for there in near + line + far:
+    for there in rest:
         pl.semaphore_signal(barrier, inc=1, device_id={"dom": there}, device_id_type=MESH)
     for there in others:
         pl.semaphore_signal(barrier, inc=1, device_id={"orb": there}, device_id_type=MESH)
@@ -121,7 +119,7 @@
     low = lane_bit((16, 128), 2)
     c2_out[...] = jnp.where(low, c2[0], c2[1])
 
-    pl.semaphore_wait(barrier, len(near) + len(line) + len(far) + len(others))
+    pl.semaphore_wait(barrier, len(rest) + len(others))
 
     def to_dom(src, dst, sends, recvs, k, there):
         return pltpu.make_async_remote_copy(
@@ -136,73 +134,77 @@
         first += [
             to_dom(fe_out.at[side], fe_in.at[1 - side], halo_send, halo_recv, side, there),
             to_dom(g.at[:, edge], gh.at[1 - side], halo_send, halo_recv, 2 + side, there),
-            to_dom(st_out.at[side], st_in.at[1 - side], halo_send, halo_recv, 4 + side, there),
         ]
-    for copy in first:
+    ahead = 1 - 2 * core
+    static = [
+        to_dom(
+            st_out.at[1 - core], st_in.at[core], halo_send, halo_recv, 4,
+            lax.rem(d + doms + ahead, doms),
+        )
+    ]
+    for n in range(1, 4):
+        place = core * (2 + n) + (1 - core) * (3 - n)
+        static.append(
+            to_dom(
+                c2_out, c2_in.at[place], wide_send, wide_recv, n,
+                lax.rem(d + doms + n * ahead, doms),
+            )
+        )
+    for copy in static[:1] + first + static[1:]:
         copy.start()
-    coarse = [to_dom(c2_out, c2_in.at[5 - k], wide_send, wide_recv, k, near[k]) for k in range(6)]
-    for copy in coarse:
-        copy.start()
-
-    def hand(block, k, there):
+
+    pair_side, odd = lax.div(chip, 2), lax.rem(chip, 2)
+    partner = 2 * (chip + 1 - 2 * odd) + core
+    across_inner = 2 * (2 - pair_side) + core
+    across_outer = 2 * (3 - 3 * pair_side) + core
+    blocks = [partner, across_inner, across_outer]
+    is_inner = (chip == 1) | (chip == 2)
+    is_outer = (chip == 0) | (chip == 3)
+
+    def hand(block, send, recv, there):
         return pltpu.make_async_remote_copy(
             src_ref=orbs.at[block], dst_ref=orbs.at[block],
-            send_sem=ag_send.at[k], recv_sem=ag_recv.at[k],
+            send_sem=ag_send.at[send], recv_sem=ag_recv.at[recv],
             device_id={"orb": there}, device_id_type=MESH,
         )
 
-    def up(n):
-        return hand(o - 2 * n, n, o + 2)
-
-    def down(n):
-        return hand(o + 2 * n, 3 + n, o - 2)
-
-    def over_up(n):
-        return hand(o - 2 * n, 6 + n, mate)
-
-    def over_down(n):
-        return hand(o + 2 * n, 9 + n, mate)
-
-    across = hand(o, 6, mate)
-
-    def open_gather():
-        across.start()
-
-        @pl.when(chip < 3)
-        def _():
-            up(0).start()
-
-        @pl.when(chip > 0)
-        def _():
-            down(0).start()
-
-    def relay(n):
-        @pl.when(chip >= n)
-        def _():
-            hand(o - 2 * n, n - 1, o + 2).wait_recv()
-            over_up(n).start()
-
-        if n < 3:
-
-            @pl.when((chip >= n) & (chip < 3))
-            def _():
-                up(n).start()
-
-        @pl.when(chip <= 3 - n)
-        def _():
-            hand(o + 2 * n, 3 + n - 1, o - 2).wait_recv()
-            over_down(n).start()
-
-        if n < 3:
-
-            @pl.when((chip <= 3 - n) & (chip > 0))
-            def _():
-                down(n).start()
-
-    open_gather()
-
+    to_mate = hand(o, 0, 3, mate)
+    to_partner = hand(o, 1, 0, partner)
+    inner_sends = [hand(o, 2, 1, across_outer), hand(o, 3, 1, across_inner)]
+    outer_sends = [hand(o, 2, 2, across_inner)]
+    relayed = hand(across_outer, 4, 2, partner)
+    taken = [hand(blocks[t], 5 + t, t, mate) for t in range(3)]
+    passed = [hand(blocks[t], 5 + t, 4 + t, mate) for t in range(3)]
+
+    @pl.when(is_outer)
+    def _():
+        outer_sends[0].start()
+
+    @pl.when(is_inner)
+    def _():
+        inner_sends[0].start()
+
+    to_partner.start()
+
+    @pl.when(is_inner)
+    def _():
+        inner_sends[1].start()
+
+    to_mate.start()
+
+    static[0].wait_recv()
+    swap = [
+        pltpu.make_async_remote_copy(
+            src_ref=st_in.at[core], dst_ref=st_in.at[core],
+            send_sem=halo_send.at[5], recv_sem=halo_recv.at[5],
+            device_id={"orb": mate}, device_id_type=MESH,
+        )
+    ]
+    swap[0].start()
     for copy in first:
         copy.wait_recv()
+
+    swap[0].wait_recv()
 
     for i in range(2):
         f[i, 1] = f[i, 1] + KINETIC * gh[0, i]
@@ -255,14 +257,22 @@
     ]
     for copy in third + second:
         copy.start()
-    relay(1)
+    for copy in static[1:]:
+        copy.wait_recv()
+    swap.append(
+        pltpu.make_async_remote_copy(
+            src_ref=c2_in.at[pl.ds(3 * core, 3)], dst_ref=c2_in.at[pl.ds(3 * core, 3)],
+            send_sem=wide_send.at[0], recv_sem=wide_recv.at[0],
+            device_id={"orb": mate}, device_id_type=MESH,
+        )
+    )
+    swap[1].start()
 
     k1, k2 = KINETIC / 4, KINETIC / 16
     both = jnp.where(even, shift[0], shift[1])
     for q in range(8):
         w1[q] = OMEGA / (c1[q] + (6.0 * k1 + both))
-    for copy in coarse:
-        copy.wait_recv()
+    swap[1].wait_recv()
     both2 = jnp.where(lane_bit((16, 128), 1), shift[0], shift[1])
     c2s = []
     for k in range(3):
@@ -297,7 +307,12 @@
     ]
     for copy in fourth + fifth:
         copy.start()
-    relay(2)
+    @pl.when(is_inner)
+    def _():
+        taken[2].wait_recv()
+        relayed.start()
+        passed[2].start()
+
     for copy in fourth:
         copy.wait_recv()
 
@@ -362,30 +377,36 @@
 
     lax.fori_loop(0, layers, sweep_last, 0)
 
-    relay(3)
-    across.wait_recv()
-    for n in range(1, 4):
-
-        @pl.when(chip >= n)
-        def _():
-            over_up(n).wait_recv()
-
-        @pl.when(chip <= 3 - n)
-        def _():
-            over_down(n).wait_recv()
-
-    def products(n, sums):
-        l, r = lax.div(n, 8), pl.ds(pl.multiple_of(lax.rem(n, 8) * 8, 8), 8)
-        u = [ea[i, l, r, :] for i in range(2)]
-        new = []
-        for j in range(16):
-            x = orbs[j // 2, j % 2, l, r, :]
-            new += [sums[2 * j + i] + x * u[i] for i in range(2)]
-        return tuple(new)
-
-    sums = lax.fori_loop(0, 64, products, (jnp.zeros((8, 128), F32),) * 32)
-    for m in range(32):
-        gram[pl.ds(m, 1), :] = jnp.sum(sums[m], axis=0, keepdims=True)
+    def intersect(q):
+        def products(n, sums):
+            l, r = lax.div(n, 8), pl.ds(pl.multiple_of(lax.rem(n, 8) * 8, 8), 8)
+            u = [ea[i, l, r, :] for i in range(2)]
+            new = []
+            for j in range(4):
+                x = orbs[2 * q + j // 2, j % 2, l, r, :]
+                new += [sums[2 * j + i] + x * u[i] for i in range(2)]
+            return tuple(new)
+
+        sums = lax.fori_loop(0, 64, products, (jnp.zeros((8, 128), F32),) * 8, unroll=4)
+        for m in range(8):
+            gram[q, pl.ds(m, 1), :] = jnp.sum(sums[m], axis=0, keepdims=True)
+
+    for t in range(2):
+        taken[t].wait_recv()
+        passed[t].start()
+    to_mate.wait_recv()
+    intersect(chip)
+    for t in range(2):
+        passed[t].wait_recv()
+        intersect(lax.div(blocks[t], 2))
+
+    @pl.when(is_outer)
+    def _():
+        taken[2].wait_recv()
+        passed[2].start()
+
+    passed[2].wait_recv()
+    intersect(lax.div(blocks[2], 2))
     diagonal = lax.broadcasted_iota(jnp.int32, (32, 128), 0) == lax.broadcasted_iota(
         jnp.int32, (32, 128), 1
     )
@@ -393,25 +414,16 @@
     def lay(column):
         return jnp.sum(jnp.where(diagonal, column, 0.0), axis=0, keepdims=True)
 
-    part1[0] = lay(jnp.sum(gram[...], axis=1, keepdims=True))
+    part[0] = lay(jnp.sum(gram[...].reshape(32, 128), axis=1, keepdims=True))
     sixth = [
-        to_dom(part1.at[0], part1.at[k], gram_send, gram_recv, k - 1, line[k - 1])
-        for k in range(1, 8)
+        to_dom(part.at[0], part.at[k], gram_send, gram_recv, k - 1, rest[k - 1])
+        for k in range(1, doms)
     ]
     for copy in sixth:
         copy.start()
     for copy in sixth:
         copy.wait_recv()
-    part2[0] = jnp.sum(part1[...], axis=0)
-    seventh = [
-        to_dom(part2.at[0], part2.at[k], sum_send, sum_recv, k - 1, far[k - 1])
-        for k in range(1, 4)
-    ]
-    for copy in seventh:
-        copy.start()
-    for copy in seventh:
-        copy.wait_recv()
-    total = jnp.sum(part2[...], axis=0) * (1.0 / cells)
+    total = jnp.sum(part[...], axis=0) * (1.0 / cells)
     coef[...] = jnp.broadcast_to(
         jnp.sum(jnp.where(diagonal, total, 0.0), axis=1, keepdims=True), (32, 128)
     )
@@ -433,41 +445,33 @@
     store = pltpu.make_async_copy(eb.at[:, pl.ds(0, layers)], out, load_sem.at[0])
     store.start()
 
-    for copy in first + coarse + third + fourth + fifth + sixth + seventh:
+    for copy in first + static + swap + third + fourth + fifth + sixth:
         copy.wait_send()
-    across.wait_send()
-    for n in range(3):
-
-        @pl.when((chip >= n) & (chip < 3))
-        def _():
-            up(n).wait_send()
-
-        @pl.when((chip <= 3 - n) & (chip > 0))
-        def _():
-            down(n).wait_send()
-
-    for n in range(1, 4):
-
-        @pl.when(chip >= n)
-        def _():
-            over_up(n).wait_send()
-
-        @pl.when(chip <= 3 - n)
-        def _():
-            over_down(n).wait_send()
+    for copy in [to_mate, to_partner] + passed:
+        copy.wait_send()
+
+    @pl.when(is_outer)
+    def _():
+        outer_sends[0].wait_send()
+
+    @pl.when(is_inner)
+    def _():
+        for copy in inner_sends + [relayed]:
+            copy.wait_send()
 
     store.wait()
 
 
 def on_device(orbitals, initial_guess, potential, perturbation, level_shifts, assignment):
-    cells = orbitals.shape[1] * lax.axis_size("dom") * orbitals.shape[2] * orbitals.shape[3]
+    doms = lax.axis_size("dom")
+    cells = orbitals.shape[1] * doms * orbitals.shape[2] * orbitals.shape[3]
     dma = pltpu.SemaphoreType.DMA
     vmem = pltpu.VMEM
 
     def field(*shape):
         return vmem(shape, F32)
 
-    anywhere = pl.BlockSpec(memory_space=pl.ANY)
+    anywhere = pl.BlockSpec(memory_space=pltpu.HBM)
     scalars = pl.BlockSpec(memory_space=pltpu.SMEM)
     return pl.pallas_call(
         functools.partial(kernel, cells),
@@ -497,24 +501,21 @@
             field(16, 128),
             field(6, 16, 128),
             field(6, 64, 128),
-            field(32, 128),
-            field(8, 1, 128),
-            field(4, 1, 128),
+            field(4, 8, 128),
+            field(doms, 1, 128),
             field(32, 128),
             dma((4,)),
             dma((12,)),
             dma((12,)),
             dma((12,)),
             dma((12,)),
-            dma((13,)),
-            dma((13,)),
+            dma((8,)),
             dma((7,)),
-            dma((7,)),
-            dma((3,)),
-            dma((3,)),
+            dma((doms - 1,)),
+            dma((doms - 1,)),
         ],
         compiler_params=pltpu.CompilerParams(
-            collective_id=0, has_side_effects=True, vmem_limit_bytes=32 << 20
+            collective_id=0, has_side_effects=True, vmem_limit_bytes=67043328
         ),
         name="sternheimer",
     )(orbitals, initial_guess, potential, perturbation, level_shifts, assignment)

time: 101 us -> 92.6 us (0.917)
  local copies, waits for them, and re-layouts: 6.09 us -> 1.89 us
  Pallas kernels: 94.5 us -> 90.6 us
    unnamed x13 -> x1, local copies, waits for them, and re-layouts: 6.09 us -> 1.89 us
    pallas_call x1, Pallas kernels: 94.5 us -> 90.6 us  [on_device(): pl.pallas_call(functools.partial(kernel, cells), out_shape=jax.ShapeDtype...]
where the time goes in v1:
time: 92.6 us; the launch traced here: 92.5 us
  Pallas kernels  90.6 us (98%)
  local copies, waits for them, and re-layouts  1.89 us (2%)
    pallas_call x1, Pallas kernels, on_device(): pl.pallas_call(functools.partial(kernel, cells), out_shape=jax.ShapeDtype...  90.6 us
    unnamed x1, local copies, waits for them, and re-layouts  1.89 us

profile of v1, /device:TPU:1, one launch (start us, length us, event | category | flops | bytes accessed | tf_op | source)
XLA Modules:
  0.0 92.5 jit_solution(756752716544821062)
XLA Ops:
  0.0 90.6 %sternheimer.1 = f32[2,8,64,128]{3,2,1,0:T(8,128)} custom-call(f32[2,8,64,128]{3,2,1,0:T(8,128)} %orb_in.1, f32[2,8,64,128]{3,2,1,0:T(8,128)} %guess_in.1, f32[8,64,128]{2,1,0:T(8,128)} %pot_in.1, f32[8,64,128]{2,1,0:T(8,128)} %pert_in.1, f32[16]{0:T(128)} %table.1, s32[2]{0:T(128)} %slot.1), custom_call_target="tpu_custom_call" | custom-call | tf_op jit(solution)/shard_map/sternheimer/pallas_call | solution.py:476
  90.6 1.9 %copy.8 = f32[2,8,64,128]{3,2,1,0:T(8,128)} copy(f32[2,8,64,128]{3,2,1,0:T(8,128)} %sternheimer.1) | data formatting | bytes 1048576

commit v2 on v1

--- a/solution.py
+++ b/solution.py
@@ -43,25 +43,16 @@
 
 
 def kernel(
-    cells, orb_in, guess_in, pot_in, pert_in, table, slot, out,
+    cells, orb_in, guess_in, pot_in, pert_in, table_in, slot_in, out,
     orbs, g, pot, pert, gh, st_out, st_in, c2_out, c2_in, fe_out, fe_in,
-    f, w, ea, eb, f1, c1, w1, e1, f2_out, f2_in, rows, gram, part, coef,
-    load_sem, halo_send, halo_recv, wide_send, wide_recv, ag_send, ag_recv,
+    f, w, ea, eb, f1, c1, w1, e1, f2_out, f2_in, rows, gram, guest, part, coef,
+    table, slot, load_sem, halo_send, halo_recv, wide_send, wide_recv, ag_send, ag_recv,
     gram_send, gram_recv,
 ):
     d = lax.axis_index("dom")
     o = lax.axis_index("orb")
     doms = lax.axis_size("dom")
     layers, half, quarter = 8, 4, 2
-
-    loads = [
-        pltpu.make_async_copy(guess_in, g.at[:, pl.ds(1, layers)], load_sem.at[0]),
-        pltpu.make_async_copy(orb_in, orbs.at[o], load_sem.at[1]),
-        pltpu.make_async_copy(pot_in, pot, load_sem.at[2]),
-        pltpu.make_async_copy(pert_in, pert, load_sem.at[3]),
-    ]
-    for copy in loads:
-        copy.start()
 
     barrier = pltpu.get_barrier_semaphore()
     near = [lax.rem(d + doms + k, doms) for k in (-3, -2, -1, 1, 2, 3)]
@@ -74,14 +65,24 @@
     for there in others:
         pl.semaphore_signal(barrier, inc=1, device_id={"orb": there}, device_id_type=MESH)
 
-    shift = [table[slot[i]] for i in range(2)]
-    base = [6.0 * KINETIC + s for s in shift]
+    loads = [
+        pltpu.make_async_copy(guess_in, g.at[:, pl.ds(1, layers)], load_sem.at[0]),
+        pltpu.make_async_copy(orb_in, orbs.at[o], load_sem.at[1]),
+        pltpu.make_async_copy(pot_in, pot, load_sem.at[2]),
+        pltpu.make_async_copy(pert_in, pert, load_sem.at[3]),
+        pltpu.make_async_copy(table_in, table, load_sem.at[4]),
+        pltpu.make_async_copy(slot_in, slot, load_sem.at[5]),
+    ]
+    for copy in loads:
+        copy.start()
     zero = jnp.zeros((64, 128), F32)
     for i in range(2):
         g[i, 0] = zero
         g[i, layers + 1] = zero
     for copy in loads:
         copy.wait()
+    shift = [table[slot[i]] for i in range(2)]
+    base = [6.0 * KINETIC + s for s in shift]
 
     def start_layer(l, carry):
         p, q = pot[l], pert[l]
@@ -153,44 +154,84 @@
     for copy in static[:1] + first + static[1:]:
         copy.start()
 
-    pair_side, odd = lax.div(chip, 2), lax.rem(chip, 2)
-    partner = 2 * (chip + 1 - 2 * odd) + core
-    across_inner = 2 * (2 - pair_side) + core
-    across_outer = 2 * (3 - 3 * pair_side) + core
-    blocks = [partner, across_inner, across_outer]
+    early, late = pl.ds(0, 6), pl.ds(6, 2)
     is_inner = (chip == 1) | (chip == 2)
     is_outer = (chip == 0) | (chip == 3)
 
-    def hand(block, send, recv, there):
+    def hand(block, h, k, there, part=pl.ds(0, 8)):
         return pltpu.make_async_remote_copy(
-            src_ref=orbs.at[block], dst_ref=orbs.at[block],
-            send_sem=ag_send.at[send], recv_sem=ag_recv.at[recv],
+            src_ref=orbs.at[block, h, part], dst_ref=orbs.at[block, h, part],
+            send_sem=ag_send.at[k], recv_sem=ag_recv.at[k],
             device_id={"orb": there}, device_id_type=MESH,
         )
 
-    to_mate = hand(o, 0, 3, mate)
-    to_partner = hand(o, 1, 0, partner)
-    inner_sends = [hand(o, 2, 1, across_outer), hand(o, 3, 1, across_inner)]
-    outer_sends = [hand(o, 2, 2, across_inner)]
-    relayed = hand(across_outer, 4, 2, partner)
-    taken = [hand(blocks[t], 5 + t, t, mate) for t in range(3)]
-    passed = [hand(blocks[t], 5 + t, 4 + t, mate) for t in range(3)]
-
-    @pl.when(is_outer)
-    def _():
-        outer_sends[0].start()
-
-    @pl.when(is_inner)
-    def _():
-        inner_sends[0].start()
-
-    to_partner.start()
-
-    @pl.when(is_inner)
-    def _():
-        inner_sends[1].start()
-
-    to_mate.start()
+    def reach(n, most):
+        return early if n == most else pl.ds(0, 8)
+
+    def up(n, h):
+        return hand(o - 2 * n, h, 2 * n + h, o + 2, reach(n, 2))
+
+    def down(n, h):
+        return hand(o + 2 * n, h, 6 + 2 * n + h, o - 2, reach(n, 2))
+
+    def share_up(n, h):
+        return hand(o - 2 * n, h, 12 + 2 * n + h, mate, reach(n, 3))
+
+    def share_down(n, h):
+        return hand(o + 2 * n, h, 18 + 2 * n + h, mate, reach(n, 3))
+
+    late_up = [hand(o - 4, h, 26 + h, o + 2, late) for h in range(2)]
+    late_down = [hand(o + 4, h, 28 + h, o - 2, late) for h in range(2)]
+    near_end = o + 2 - 4 * lax.rem(chip, 2)
+    far = 2 * (3 - 3 * lax.div(chip, 2)) + core
+    late_share = [hand(far, h, 30 + h, mate, late) for h in range(2)]
+    visit = pltpu.make_async_remote_copy(
+        src_ref=ea.at[:, late], dst_ref=guest,
+        send_sem=ag_send.at[32], recv_sem=ag_recv.at[32],
+        device_id={"orb": near_end}, device_id_type=MESH,
+    )
+    answer = pltpu.make_async_remote_copy(
+        src_ref=gram.at[4], dst_ref=gram.at[5],
+        send_sem=ag_send.at[33], recv_sem=ag_recv.at[33],
+        device_id={"orb": near_end}, device_id_type=MESH,
+    )
+    own = [hand(o, h, 12 + h, mate) for h in range(2)]
+
+    def relay(n, h):
+        @pl.when(chip >= n)
+        def _():
+            hand(o - 2 * n, h, 2 * (n - 1) + h, mate, reach(n, 3)).wait_recv()
+            if n < 3:
+
+                @pl.when(chip < 3)
+                def _():
+                    up(n, h).start()
+
+            share_up(n, h).start()
+
+        @pl.when(chip <= 3 - n)
+        def _():
+            hand(o + 2 * n, h, 6 + 2 * (n - 1) + h, mate, reach(n, 3)).wait_recv()
+            if n < 3:
+
+                @pl.when(chip > 0)
+                def _():
+                    down(n, h).start()
+
+            share_down(n, h).start()
+
+    for h in range(2):
+
+        @pl.when(chip < 3)
+        def _():
+            up(0, h).start()
+
+        @pl.when(chip > 0)
+        def _():
+            down(0, h).start()
+
+    for copy in own:
+        copy.start()
 
     static[0].wait_recv()
     swap = [
@@ -307,12 +348,8 @@
     ]
     for copy in fourth + fifth:
         copy.start()
-    @pl.when(is_inner)
-    def _():
-        taken[2].wait_recv()
-        relayed.start()
-        passed[2].start()
-
+    relay(1, 0)
+    relay(1, 1)
     for copy in fourth:
         copy.wait_recv()
 
@@ -343,6 +380,8 @@
         rows[q, pl.ds(0, 32, stride=2)] = e[q]
         rows[q, pl.ds(1, 32, stride=2)] = e[q]
 
+    relay(2, 0)
+
     for copy in second:
         copy.wait_recv()
 
@@ -375,38 +414,90 @@
             )
         return carry
 
-    lax.fori_loop(0, layers, sweep_last, 0)
-
-    def intersect(q):
+    lax.fori_loop(layers - 2, layers, sweep_last, 0)
+
+    @pl.when(is_outer)
+    def _():
+        visit.start()
+
+    lax.fori_loop(0, layers - 2, sweep_last, 0)
+    relay(2, 1)
+
+    def intersect(q, h, start, stop):
         def products(n, sums):
             l, r = lax.div(n, 8), pl.ds(pl.multiple_of(lax.rem(n, 8) * 8, 8), 8)
             u = [ea[i, l, r, :] for i in range(2)]
             new = []
-            for j in range(4):
-                x = orbs[2 * q + j // 2, j % 2, l, r, :]
-                new += [sums[2 * j + i] + x * u[i] for i in range(2)]
+            for c in range(2):
+                x = orbs[2 * q + c, h, l, r, :]
+                new += [sums[2 * c + i] + x * u[i] for i in range(2)]
             return tuple(new)
 
-        sums = lax.fori_loop(0, 64, products, (jnp.zeros((8, 128), F32),) * 8, unroll=4)
+        sums = lax.fori_loop(start, stop, products, (jnp.zeros((8, 128), F32),) * 4, unroll=8)
+        for m in range(4):
+            row = pl.ds(4 * (m // 2) + 2 * h + m % 2, 1)
+            found = jnp.sum(sums[m], axis=0, keepdims=True)
+            gram[q, row, :] = found
+
+    pair_side, odd = lax.div(chip, 2), lax.rem(chip, 2)
+    ways = [
+        (chip + 1 - 2 * odd, 1 - odd),
+        (2 - pair_side, 1 - pair_side),
+        (3 - 3 * pair_side, 1 - pair_side),
+    ]
+    for copy in own:
+        copy.wait_recv()
+    for h in range(2):
+        intersect(chip, h, 0, 64)
+    for n, (q, is_down) in enumerate(ways):
+        away = (q - chip) * (2 * is_down - 1)
+        slot_of = 12 + 6 * is_down + 2 * away
+        block = 2 * q + 1 - core
+        for h in range(2):
+            if n < 2:
+                hand(block, h, slot_of + h, mate).wait_recv()
+                intersect(q, h, 0, 64)
+                continue
+            relay(3, h)
+
+            @pl.when(is_outer)
+            def _():
+                hand(block, h, slot_of + h, mate, early).wait_recv()
+
+            @pl.when(is_inner)
+            def _():
+                hand(block, h, slot_of + h, mate).wait_recv()
+                intersect(q, h, 0, 64)
+
+            @pl.when(is_outer)
+            def _():
+                intersect(q, h, 0, 48)
+
+    @pl.when(is_inner)
+    def _():
+        visit.wait_recv()
+
+        def products(n, sums):
+            l, r = lax.div(n, 8), pl.ds(pl.multiple_of(lax.rem(n, 8) * 8, 8), 8)
+            u = [guest[i, l, r, :] for i in range(2)]
+            new = []
+            for c in range(2):
+                for h in range(2):
+                    x = orbs[far - core + c, h, 6 + l, r, :]
+                    new += [sums[len(new) + i] + x * u[i] for i in range(2)]
+            return tuple(new)
+
+        sums = lax.fori_loop(0, 16, products, (jnp.zeros((8, 128), F32),) * 8, unroll=4)
         for m in range(8):
-            gram[q, pl.ds(m, 1), :] = jnp.sum(sums[m], axis=0, keepdims=True)
-
-    for t in range(2):
-        taken[t].wait_recv()
-        passed[t].start()
-    to_mate.wait_recv()
-    intersect(chip)
-    for t in range(2):
-        passed[t].wait_recv()
-        intersect(lax.div(blocks[t], 2))
+            gram[4, pl.ds(m, 1), :] = jnp.sum(sums[m], axis=0, keepdims=True)
+        answer.start()
 
     @pl.when(is_outer)
     def _():
-        taken[2].wait_recv()
-        passed[2].start()
-
-    passed[2].wait_recv()
-    intersect(lax.div(blocks[2], 2))
+        answer.wait_recv()
+        last = 3 - 3 * lax.div(chip, 2)
+        gram[last] = gram[last] + gram[5]
+
     diagonal = lax.broadcasted_iota(jnp.int32, (32, 128), 0) == lax.broadcasted_iota(
         jnp.int32, (32, 128), 1
     )
@@ -414,13 +505,24 @@
     def lay(column):
         return jnp.sum(jnp.where(diagonal, column, 0.0), axis=0, keepdims=True)
 
-    part[0] = lay(jnp.sum(gram[...].reshape(32, 128), axis=1, keepdims=True))
+    part[0] = lay(jnp.sum(gram[pl.ds(0, 4)].reshape(32, 128), axis=1, keepdims=True))
     sixth = [
         to_dom(part.at[0], part.at[k], gram_send, gram_recv, k - 1, rest[k - 1])
         for k in range(1, doms)
     ]
     for copy in sixth:
         copy.start()
+
+    @pl.when(chip == 2)
+    def _():
+        for copy in late_up:
+            copy.start()
+
+    @pl.when(chip == 1)
+    def _():
+        for copy in late_down:
+            copy.start()
+
     for copy in sixth:
         copy.wait_recv()
     total = jnp.sum(part[...], axis=0) * (1.0 / cells)
@@ -441,25 +543,81 @@
             eb[i, l, r, :] = ea[i, l, r, :] - lost[i]
         return carry
 
-    lax.fori_loop(0, 64, project, 0)
-    store = pltpu.make_async_copy(eb.at[:, pl.ds(0, layers)], out, load_sem.at[0])
-    store.start()
+    for h in range(2):
+
+        @pl.when(chip == 3)
+        def _():
+            hand(far, h, 26 + h, mate, late).wait_recv()
+
+        @pl.when(chip == 0)
+        def _():
+            hand(far, h, 28 + h, mate, late).wait_recv()
+
+    @pl.when(is_outer)
+    def _():
+        for copy in late_share:
+            copy.start()
+
+    stores = []
+    for k in range(4):
+        if k == 3:
+
+            @pl.when(is_outer)
+            def _():
+                for h in range(2):
+                    hand(far + 1 - 2 * core, h, 30 + h, mate, late).wait_recv()
+
+        lax.fori_loop(16 * k, 16 * k + 16, project, 0, unroll=2)
+        part_of = pl.ds(2 * k, 2)
+        stores.append(pltpu.make_async_copy(eb.at[:, part_of], out.at[:, part_of], load_sem.at[k]))
+        stores[k].start()
 
     for copy in first + static + swap + third + fourth + fifth + sixth:
         copy.wait_send()
-    for copy in [to_mate, to_partner] + passed:
+    for copy in own:
         copy.wait_send()
+    for h in range(2):
+        for n in range(3):
+
+            @pl.when((chip >= n) & (chip < 3))
+            def _():
+                up(n, h).wait_send()
+
+            @pl.when((chip <= 3 - n) & (chip > 0))
+            def _():
+                down(n, h).wait_send()
+
+        for n in range(1, 4):
+
+            @pl.when(chip >= n)
+            def _():
+                share_up(n, h).wait_send()
+
+            @pl.when(chip <= 3 - n)
+            def _():
+                share_down(n, h).wait_send()
 
     @pl.when(is_outer)
     def _():
-        outer_sends[0].wait_send()
+        for copy in late_share + [visit]:
+            copy.wait_send()
 
     @pl.when(is_inner)
     def _():
-        for copy in inner_sends + [relayed]:
+        answer.wait_send()
+
+    @pl.when(chip == 2)
+    def _():
+        for copy in late_up:
             copy.wait_send()
 
-    store.wait()
+    @pl.when(chip == 1)
+    def _():
+        for copy in late_down:
+            copy.wait_send()
+
+    for store in stores:
+        store.wait()
 
 
 def on_device(orbitals, initial_guess, potential, perturbation, level_shifts, assignment):
@@ -472,11 +630,10 @@
         return vmem(shape, F32)
 
     anywhere = pl.BlockSpec(memory_space=pltpu.HBM)
-    scalars = pl.BlockSpec(memory_space=pltpu.SMEM)
     return pl.pallas_call(
         functools.partial(kernel, cells),
         out_shape=jax.ShapeDtypeStruct(orbitals.shape, F32),
-        in_specs=[anywhere] * 4 + [scalars] * 2,
+        in_specs=[anywhere] * 6,
         out_specs=anywhere,
         scratch_shapes=[
             field(8, 2, 8, 64, 128),
@@ -501,16 +658,19 @@
             field(16, 128),
             field(6, 16, 128),
             field(6, 64, 128),
-            field(4, 8, 128),
+            field(6, 8, 128),
+            field(2, 2, 64, 128),
             field(doms, 1, 128),
             field(32, 128),
-            dma((4,)),
+            pltpu.SMEM((16,), F32),
+            pltpu.SMEM((2,), jnp.int32),
+            dma((6,)),
             dma((12,)),
             dma((12,)),
             dma((12,)),
             dma((12,)),
-            dma((8,)),
-            dma((7,)),
+            dma((34,)),
+            dma((34,)),
             dma((doms - 1,)),
             dma((doms - 1,)),
         ],

time: 92.6 us -> 90.4 us (0.976)
  Pallas kernels: 90.6 us -> 88.4 us
    pallas_call x1, Pallas kernels: 90.6 us -> 88.4 us  [on_device(): pl.pallas_call(functools.partial(kernel, cells), out_shape=jax.ShapeDtype...]
where the time goes in v2:
time: 90.4 us; the launch traced here: 90.3 us
  Pallas kernels  88.4 us (98%)
  local copies, waits for them, and re-layouts  1.89 us (2%)
    pallas_call x1, Pallas kernels, on_device(): pl.pallas_call(functools.partial(kernel, cells), out_shape=jax.ShapeDtype...  88.4 us
    unnamed x1, local copies, waits for them, and re-layouts  1.89 us

profile of v2, /device:TPU:1, one launch (start us, length us, event | category | flops | bytes accessed | tf_op | source)
XLA Modules:
  0.0 90.3 jit_solution(16302490579036315101)
XLA Ops:
  0.0 88.4 %sternheimer.1 = f32[2,8,64,128]{3,2,1,0:T(8,128)} custom-call(f32[2,8,64,128]{3,2,1,0:T(8,128)} %orb_in.1, f32[2,8,64,128]{3,2,1,0:T(8,128)} %guess_in.1, f32[8,64,128]{2,1,0:T(8,128)} %pot_in.1, f32[8,64,128]{2,1,0:T(8,128)} %pert_in.1, f32[16]{0:T(128)} %table_in.1, s32[2]{0:T(128)} %slot_in.1), custom_call_target="tpu_custom_call" | custom-call | tf_op jit(solution)/shard_map/sternheimer/pallas_call | solution.py:633
  88.4 1.9 %copy.8 = f32[2,8,64,128]{3,2,1,0:T(8,128)} copy(f32[2,8,64,128]{3,2,1,0:T(8,128)} %sternheimer.1) | data formatting | bytes 1048576

commit v3 on v2

--- a/solution.py
+++ b/solution.py
@@ -8,6 +8,7 @@
 from jax.sharding import PartitionSpec as P
 
 OMEGA = 0.8
+LATE = 4
 KINETIC = 8.0
 MESH = pl.DeviceIdType.MESH
 F32 = jnp.float32
@@ -154,7 +155,8 @@
     for copy in static[:1] + first + static[1:]:
         copy.start()
 
-    early, late = pl.ds(0, 6), pl.ds(6, 2)
+    cut = layers - LATE
+    early, late = pl.ds(0, cut), pl.ds(cut, LATE)
     is_inner = (chip == 1) | (chip == 2)
     is_outer = (chip == 0) | (chip == 3)
 
@@ -414,14 +416,13 @@
             )
         return carry
 
-    lax.fori_loop(layers - 2, layers, sweep_last, 0)
+    lax.fori_loop(cut, layers, sweep_last, 0)
 
     @pl.when(is_outer)
     def _():
         visit.start()
 
-    lax.fori_loop(0, layers - 2, sweep_last, 0)
-    relay(2, 1)
+    lax.fori_loop(0, cut, sweep_last, 0)
 
     def intersect(q, h, start, stop):
         def products(n, sums):
@@ -454,6 +455,8 @@
         slot_of = 12 + 6 * is_down + 2 * away
         block = 2 * q + 1 - core
         for h in range(2):
+            if n == 1 and h == 1:
+                relay(2, 1)
             if n < 2:
                 hand(block, h, slot_of + h, mate).wait_recv()
                 intersect(q, h, 0, 64)
@@ -471,7 +474,7 @@
 
             @pl.when(is_outer)
             def _():
-                intersect(q, h, 0, 48)
+                intersect(q, h, 0, 8 * cut)
 
     @pl.when(is_inner)
     def _():
@@ -483,11 +486,11 @@
             new = []
             for c in range(2):
                 for h in range(2):
-                    x = orbs[far - core + c, h, 6 + l, r, :]
+                    x = orbs[far - core + c, h, cut + l, r, :]
                     new += [sums[len(new) + i] + x * u[i] for i in range(2)]
             return tuple(new)
 
-        sums = lax.fori_loop(0, 16, products, (jnp.zeros((8, 128), F32),) * 8, unroll=4)
+        sums = lax.fori_loop(0, 8 * LATE, products, (jnp.zeros((8, 128), F32),) * 8, unroll=4)
         for m in range(8):
             gram[4, pl.ds(m, 1), :] = jnp.sum(sums[m], axis=0, keepdims=True)
         answer.start()
@@ -559,16 +562,17 @@
             copy.start()
 
     stores = []
+    bounds = [0, 2, cut, layers - 1, layers]
     for k in range(4):
-        if k == 3:
+        if k == 2:
 
             @pl.when(is_outer)
             def _():
                 for h in range(2):
                     hand(far + 1 - 2 * core, h, 30 + h, mate, late).wait_recv()
 
-        lax.fori_loop(16 * k, 16 * k + 16, project, 0, unroll=2)
-        part_of = pl.ds(2 * k, 2)
+        lax.fori_loop(8 * bounds[k], 8 * bounds[k + 1], project, 0, unroll=2)
+        part_of = pl.ds(bounds[k], bounds[k + 1] - bounds[k])
         stores.append(pltpu.make_async_copy(eb.at[:, part_of], out.at[:, part_of], load_sem.at[k]))
         stores[k].start()
 
@@ -659,7 +663,7 @@
             field(6, 16, 128),
             field(6, 64, 128),
             field(6, 8, 128),
-            field(2, 2, 64, 128),
+            field(2, LATE, 64, 128),
             field(doms, 1, 128),
             field(32, 128),
             pltpu.SMEM((16,), F32),

time: 90.4 us -> 87.7 us (0.970)
  Pallas kernels: 88.4 us -> 85.7 us
    pallas_call x1, Pallas kernels: 88.4 us -> 85.7 us  [on_device(): pl.pallas_call(functools.partial(kernel, cells), out_shape=jax.ShapeDtype...]
where the time goes in v3:
time: 87.7 us; the launch traced here: 87.5 us
  Pallas kernels  85.7 us (98%)
  local copies, waits for them, and re-layouts  1.89 us (2%)
    pallas_call x1, Pallas kernels, on_device(): pl.pallas_call(functools.partial(kernel, cells), out_shape=jax.ShapeDtype...  85.7 us
    unnamed x1, local copies, waits for them, and re-layouts  1.89 us

profile of v3, /device:TPU:1, one launch (start us, length us, event | category | flops | bytes accessed | tf_op | source)
XLA Modules:
  0.0 87.5 jit_solution(16621297453407946403)
XLA Ops:
  0.0 85.7 %sternheimer.1 = f32[2,8,64,128]{3,2,1,0:T(8,128)} custom-call(f32[2,8,64,128]{3,2,1,0:T(8,128)} %orb_in.1, f32[2,8,64,128]{3,2,1,0:T(8,128)} %guess_in.1, f32[8,64,128]{2,1,0:T(8,128)} %pot_in.1, f32[8,64,128]{2,1,0:T(8,128)} %pert_in.1, f32[16]{0:T(128)} %table_in.1, s32[2]{0:T(128)} %slot_in.1), custom_call_target="tpu_custom_call" | custom-call | tf_op jit(solution)/shard_map/sternheimer/pallas_call | solution.py:637
  85.7 1.9 %copy.8 = f32[2,8,64,128]{3,2,1,0:T(8,128)} copy(f32[2,8,64,128]{3,2,1,0:T(8,128)} %sternheimer.1) | data formatting | bytes 1048576

commit v4 on v3

--- a/solution.py
+++ b/solution.py
@@ -95,7 +95,7 @@
             w[i, l + 1] = OMEGA / diag
         return carry
 
-    lax.fori_loop(0, layers, start_layer, 0)
+    lax.fori_loop(0, layers, start_layer, 0, unroll=2)
     for side, (edge, inner) in enumerate(((1, 2), (layers, layers - 1))):
         for i in range(2):
             fe_out[side, 0, i] = f[i, edge]
@@ -264,7 +264,7 @@
             ea[i, l + 1] = w[i, l] * f[i, l]
         return carry
 
-    lax.fori_loop(0, layers + 2, begin, 0)
+    lax.fori_loop(0, layers + 2, begin, 0, unroll=2)
 
     def sweep_down(l, carry):
         for i in range(2):
@@ -272,7 +272,7 @@
             eb[i, l + 1] = w[i, l] * ((2.0 - OMEGA) * f[i, l] + KINETIC * around)
         return carry
 
-    lax.fori_loop(0, layers + 2, sweep_down, 0)
+    lax.fori_loop(0, layers + 2, sweep_down, 0, unroll=2)
     second = [
         to_dom(eb.at[:, 3], eb.at[:, 11], halo_send, halo_recv, 6, below),
         to_dom(eb.at[:, 8], eb.at[:, 0], halo_send, halo_recv, 7, above),
@@ -291,7 +291,7 @@
         rows[q] = pair(total[0], total[1], 1)
         return carry
 
-    lax.fori_loop(0, half, remainder, 0)
+    lax.fori_loop(0, half, remainder, 0, unroll=2)
     for q in range(half):
         f1[q + 2] = 0.125 * (rows[q, pl.ds(0, 32, stride=2)] + rows[q, pl.ds(1, 32, stride=2)])
     third = [
@@ -394,7 +394,7 @@
                 ea[i, 2 * q + h] = eb[i, 2 * q + h] + fields[i]
         return carry
 
-    lax.fori_loop(0, 6, correct, 0)
+    lax.fori_loop(0, 6, correct, 0, unroll=2)
     for copy in second:
         copy.wait_send()
 
@@ -405,7 +405,7 @@
             eb[i, l + 1] = (1.0 - OMEGA) * x + w[i, l] * (f[i, l] + KINETIC * around)
         return carry
 
-    lax.fori_loop(0, layers + 2, sweep_up, 0)
+    lax.fori_loop(0, layers + 2, sweep_up, 0, unroll=2)
 
     def sweep_last(l, carry):
         for i in range(2):
@@ -416,13 +416,13 @@
             )
         return carry
 
-    lax.fori_loop(cut, layers, sweep_last, 0)
+    lax.fori_loop(cut, layers, sweep_last, 0, unroll=2)
 
     @pl.when(is_outer)
     def _():
         visit.start()
 
-    lax.fori_loop(0, cut, sweep_last, 0)
+    lax.fori_loop(0, cut, sweep_last, 0, unroll=2)
 
     def intersect(q, h, start, stop):
         def products(n, sums):
@@ -526,6 +526,18 @@
         for copy in late_down:
             copy.start()
 
+    for h in range(2):
+
+        @pl.when(chip == 3)
+        def _():
+            hand(far, h, 26 + h, mate, late).wait_recv()
+            late_share[h].start()
+
+        @pl.when(chip == 0)
+        def _():
+            hand(far, h, 28 + h, mate, late).wait_recv()
+            late_share[h].start()
+
     for copy in sixth:
         copy.wait_recv()
     total = jnp.sum(part[...], axis=0) * (1.0 / cells)
@@ -545,21 +557,6 @@
         for i in range(2):
             eb[i, l, r, :] = ea[i, l, r, :] - lost[i]
         return carry
-
-    for h in range(2):
-
-        @pl.when(chip == 3)
-        def _():
-            hand(far, h, 26 + h, mate, late).wait_recv()
-
-        @pl.when(chip == 0)
-        def _():
-            hand(far, h, 28 + h, mate, late).wait_recv()
-
-    @pl.when(is_outer)
-    def _():
-        for copy in late_share:
-            copy.start()
 
     stores = []
     bounds = [0, 2, cut, layers - 1, layers]

time: 87.7 us -> 87.3 us (level)
  no operation moved by 1% of the time
where the time goes in v4:
time: 87.3 us; the launch traced here: 87.1 us
  Pallas kernels  85.2 us (98%)
  local copies, waits for them, and re-layouts  1.89 us (2%)
    pallas_call x1, Pallas kernels, on_device(): pl.pallas_call(functools.partial(kernel, cells), out_shape=jax.ShapeDtype...  85.2 us
    unnamed x1, local copies, waits for them, and re-layouts  1.89 us

profile of v4, /device:TPU:1, one launch (start us, length us, event | category | flops | bytes accessed | tf_op | source)
XLA Modules:
  0.0 87.1 jit_solution(15197379739093037631)
XLA Ops:
  0.0 85.2 %sternheimer.1 = f32[2,8,64,128]{3,2,1,0:T(8,128)} custom-call(f32[2,8,64,128]{3,2,1,0:T(8,128)} %orb_in.1, f32[2,8,64,128]{3,2,1,0:T(8,128)} %guess_in.1, f32[8,64,128]{2,1,0:T(8,128)} %pot_in.1, f32[8,64,128]{2,1,0:T(8,128)} %pert_in.1, f32[16]{0:T(128)} %table_in.1, s32[2]{0:T(128)} %slot_in.1), custom_call_target="tpu_custom_call" | custom-call | tf_op jit(solution)/shard_map/sternheimer/pallas_call | solution.py:634
  85.2 1.9 %copy.8 = f32[2,8,64,128]{3,2,1,0:T(8,128)} copy(f32[2,8,64,128]{3,2,1,0:T(8,128)} %sternheimer.1) | data formatting | bytes 1048576

commit v5 on v4

--- a/solution.py
+++ b/solution.py
@@ -232,9 +232,6 @@
         def _():
             down(0, h).start()
 
-    for copy in own:
-        copy.start()
-
     static[0].wait_recv()
     swap = [
         pltpu.make_async_remote_copy(
@@ -248,6 +245,9 @@
         copy.wait_recv()
 
     swap[0].wait_recv()
+
+    for copy in own:
+        copy.start()
 
     for i in range(2):
         f[i, 1] = f[i, 1] + KINETIC * gh[0, i]

time: 87.3 us -> 87.3 us (level)
  no operation moved by 1% of the time
where the time goes in v5:
time: 87.3 us; the launch traced here: 87.1 us
  Pallas kernels  85.2 us (98%)
  local copies, waits for them, and re-layouts  1.89 us (2%)
    pallas_call x1, Pallas kernels, on_device(): pl.pallas_call(functools.partial(kernel, cells), out_shape=jax.ShapeDtype...  85.2 us
    unnamed x1, local copies, waits for them, and re-layouts  1.89 us

profile of v5, /device:TPU:1, one launch (start us, length us, event | category | flops | bytes accessed | tf_op | source)
XLA Modules:
  0.0 87.1 jit_solution(11662297249096272307)
XLA Ops:
  0.0 85.2 %sternheimer.1 = f32[2,8,64,128]{3,2,1,0:T(8,128)} custom-call(f32[2,8,64,128]{3,2,1,0:T(8,128)} %orb_in.1, f32[2,8,64,128]{3,2,1,0:T(8,128)} %guess_in.1, f32[8,64,128]{2,1,0:T(8,128)} %pot_in.1, f32[8,64,128]{2,1,0:T(8,128)} %pert_in.1, f32[16]{0:T(128)} %table_in.1, s32[2]{0:T(128)} %slot_in.1), custom_call_target="tpu_custom_call" | custom-call | tf_op jit(solution)/shard_map/sternheimer/pallas_call | solution.py:634
  85.2 1.9 %copy.8 = f32[2,8,64,128]{3,2,1,0:T(8,128)} copy(f32[2,8,64,128]{3,2,1,0:T(8,128)} %sternheimer.1) | data formatting | bytes 1048576
